TPU v7x, 256 devices: a 2x2x32 block of a 4x8x32 slice. The times are simulated.
256 devices in a mesh: member: 4 (over y, x), node: 64 (over z, core).
Axes of the slice: x: 2, y: 2, z: 32, core: 2. Of those that a mesh axis runs over, the one named last changes fastest.
The devices are a block of a 4x8x32 slice.
Arguments:
- conditioning: bfloat16 [168, 262144], P(None, ('member', 'node')), parts along dimension 1, may hold values from -6 to 6
- target_state: float32 [84, 262144], P(None, ('member', 'node')), parts along dimension 1, may hold values from -6 to 6
- noise_sample: float32 [84, 262144], P(None, ('member', 'node')), parts along dimension 1, may hold values from -6 to 6
- step_index: int32 [4], P('member'), parts along dimension 0, may hold values from 0 to 19
- mesh_features: float32 [3, 40960], P(None, 'node'), may hold values from -1 to 1
- edge_geometry: float32 [4, 262144], P(None, 'node'), may hold values from -6 to 6
- edge_slot: int32 [262144], P('node'), may hold values from 0 to 1023, as said below
- edge_receiver: int32 [262144], P('node'), may hold values from 0 to 639
- send_rows: int32 [4096, 16], P('node'), may hold values from 0 to 1023
- edge_count: int32 [64], P('node'), may hold values from 1503 to 4096, as said below
- embed_weight: bfloat16 [252, 512], replicated, may hold values from -0.375 to 0.375
- mesh_weight: float32 [3, 512], replicated, may hold values from -3.5 to 3.5
- geom_weight: float32 [4, 512], replicated, may hold values from -3 to 3
- sender_weight: bfloat16 [512, 512], P('node'), may hold values from -0.15625 to 0.15625
- edge_weight: bfloat16 [512, 512], P('node'), may hold values from -0.15625 to 0.15625
- receiver_weight: bfloat16 [512, 512], P('node'), may hold values from -0.15625 to 0.15625
- message_weight: bfloat16 [512, 512], P('node'), may hold values from -0.25 to 0.25
- node_weight: bfloat16 [1024, 512], P('node'), may hold values from -0.1875 to 0.1875
- output_weight: bfloat16 [512, 512], P('node'), may hold values from -0.25 to 0.25
- noise_weight: float32 [32, 512], replicated, may hold values from -1 to 1
- film_weight: bfloat16 [512, 2048], replicated, may hold values from -0.25 to 0.25
Outputs:
- mesh_latent: bfloat16 [40960, 2048], P('node', 'member'), parts along dimension 1
There are 4 independent parts, one for each index of `member`. A program takes and returns all parts, laid end to end along the dimension named above; an argument that names none is the same for every part. Nothing has to cross between parts.
Inputs may be any that keep to these rules, and one draw needn't show every extreme that they name: `edge_slot`: on each device, the live slots name every entry of its 64 * 16 list at least once, or as many distinct entries as there are live slots where these are fewer. `edge_count`: the counts sum to 64 * 2048 and one device has all 4096 slots live.
All inputs are finite; a program needn't handle non-finite values.
Results may differ from a plain program's by a relative error of at most 0.0071.
Values may be sent and summed in bfloat16 or wider, within the bound.
No kernel may reach another device: no remote copies, remote signals or barrier semaphores. Data moves between devices by JAX's collectives and lax.ppermute only.
A program may use at most 64 MiB of HBM per device.

v0:
```python
import jax
import jax.numpy as jnp
from jax import lax
from jax.sharding import PartitionSpec as P

STEPS = 20
sigma_top = 80.0
sigma_low = 0.03
rho_power = 7.0
norm_eps = 1e-05


def in_one_piece(arrays, axis, dim, along):
    widths = [a.shape[along] for a in arrays]
    both = jnp.concatenate(arrays, axis=along)
    out = lax.all_gather(both, axis, axis=dim, tiled=True)
    return tuple(jnp.split(out, [sum(widths[:k]) for k in range(1, len(widths))], axis=along))


def layer_norm(values):
    mean = jnp.mean(values, axis=-1, keepdims=True)
    centred = values - mean
    var = jnp.mean(centred * centred, axis=-1, keepdims=True)
    return centred * lax.rsqrt(var + norm_eps)


def embed_columns(inputs, embed_weight):
    product = lax.dot_general(
        inputs, embed_weight, (((0,), (0,)), ((), ())), preferred_element_type=jnp.float32
    )
    return jax.nn.silu(product).astype(jnp.bfloat16)


def per_device(
    conditioning,
    target_state,
    noise_sample,
    step_index,
    mesh_features,
    edge_geometry,
    edge_slot,
    edge_receiver,
    send_rows,
    edge_count,
    embed_weight,
    mesh_weight,
    geom_weight,
    sender_weight,
    edge_weight,
    receiver_weight,
    message_weight,
    node_weight,
    output_weight,
    noise_weight,
    film_weight,
):
    width = embed_weight.shape[1]
    freqs = noise_weight.shape[0] // 2
    steps_total = STEPS
    frac = step_index[0].astype(jnp.float32) / (steps_total - 1)
    upper = sigma_top ** (1.0 / rho_power)
    lower = sigma_low ** (1.0 / rho_power)
    sigma = (upper + frac * (lower - upper)) ** rho_power
    angle = 0.25 * jnp.log(sigma) * (jnp.arange(freqs, dtype=jnp.float32) + 1.0)
    fourier = jnp.concatenate([jnp.sin(angle), jnp.cos(angle)])[None, :]
    cond = jax.nn.silu(jnp.dot(fourier, noise_weight, precision=lax.Precision.HIGHEST)).astype(
        jnp.bfloat16
    )
    film = jnp.dot(cond, film_weight, preferred_element_type=jnp.float32)
    edge_scale = film[:, 0:width]
    edge_shift = film[:, width : 2 * width]
    node_scale = film[:, 2 * width : 3 * width]
    node_shift = film[:, 3 * width : 4 * width]
    full_sender, full_edge, full_recv, full_message, full_node, full_output = (
        *in_one_piece((sender_weight, edge_weight, receiver_weight, message_weight), "node", 0, 1),
        lax.all_gather(node_weight, "node", axis=0, tiled=True),
        lax.all_gather(output_weight, "node", axis=0, tiled=True),
    )
    noisy = ((target_state + sigma * noise_sample) / jnp.sqrt(sigma * sigma + 1.0)).astype(
        jnp.bfloat16
    )
    raw_local = jnp.concatenate([conditioning, noisy], axis=0)
    picked_rows = send_rows.reshape(-1)
    outgoing_inputs = raw_local[:, picked_rows]
    arrived = lax.all_to_all(outgoing_inputs, "node", split_axis=1, concat_axis=1, tiled=True)
    received = embed_columns(arrived, embed_weight)
    mesh_embed = jax.nn.silu(
        jnp.dot(mesh_features.T, mesh_weight, precision=lax.Precision.HIGHEST)
    ).astype(jnp.bfloat16)
    recv_proj = jnp.dot(mesh_embed, full_recv, preferred_element_type=jnp.float32).astype(
        jnp.bfloat16
    )
    mesh_count = mesh_embed.shape[0]
    slot_count = edge_slot.shape[0]
    block = min(512, slot_count)
    node_ids = jnp.arange(mesh_count, dtype=jnp.int32)
    count = edge_count[0]
    live_blocks = (count + block - 1) // block

    def add_block(index, total):
        start = (index * block).astype(jnp.int32)
        slots = lax.dynamic_slice_in_dim(edge_slot, start, block, 0)
        local_recv = lax.dynamic_slice_in_dim(edge_receiver, start, block, 0)
        geometry = lax.dynamic_slice_in_dim(edge_geometry, start, block, 1)
        embed_rows = jax.nn.silu(
            jnp.dot(geometry.T, geom_weight, precision=lax.Precision.HIGHEST)
        ).astype(jnp.bfloat16)
        one_hot = (local_recv[:, None] == node_ids[None, :]).astype(jnp.bfloat16)
        sender_rows = received[slots]
        pre = jnp.dot(embed_rows, full_edge, preferred_element_type=jnp.float32)
        pre = pre + jnp.dot(sender_rows, full_sender, preferred_element_type=jnp.float32)
        pre = pre + jnp.dot(one_hot, recv_proj, preferred_element_type=jnp.float32)
        hidden = jax.nn.silu(pre).astype(jnp.bfloat16)
        mixed = jnp.dot(hidden, full_message, preferred_element_type=jnp.float32)
        message = layer_norm(mixed) * (1.0 + edge_scale) + edge_shift
        live = start + jnp.arange(block, dtype=jnp.int32) < count
        message = jnp.where(live[:, None], message, 0.0).astype(jnp.bfloat16)
        return total + lax.dot_general(
            one_hot, message, (((0,), (0,)), ((), ())), preferred_element_type=jnp.float32
        )

    zeros_total = jnp.zeros((mesh_count, width), jnp.float32)
    summed = lax.fori_loop(0, live_blocks, add_block, zeros_total)
    gathered = summed.astype(jnp.bfloat16)
    joined = jnp.concatenate([mesh_embed, gathered], axis=1)
    update = jax.nn.silu(jnp.dot(joined, full_node, preferred_element_type=jnp.float32)).astype(
        jnp.bfloat16
    )
    result = jnp.dot(update, full_output, preferred_element_type=jnp.float32)
    return (
        mesh_embed.astype(jnp.float32) + layer_norm(result) * (1.0 + node_scale) + node_shift
    ).astype(jnp.bfloat16)


def solution(mesh):
    placed = (
        P(None, ("member", "node")),
        P(None, ("member", "node")),
        P(None, ("member", "node")),
        P("member"),
        P(None, "node"),
        P(None, "node"),
        P("node"),
        P("node"),
        P("node", None),
        P("node"),
        P(),
        P(),
        P(),
        P("node", None),
        P("node", None),
        P("node", None),
        P("node", None),
        P("node", None),
        P("node", None),
        P(),
        P(),
    )
    return jax.shard_map(
        per_device, mesh=mesh, in_specs=placed, out_specs=P("node", "member"), check_vma=False
    )
```

profile of v0, /device:TPU:1325, one launch (start us, length us, event | category | flops | bytes accessed | tf_op | source)
XLA Modules:
  0.0 331.0 jit_solution(2038196896726926414)
XLA Ops:
  10.8 5.0 %gather_fusion.1 = bf16[1024,252]{1,0:T(8,128)(2,1)} fusion(bf16[252,1024]{0,1:T(8,128)(2,1)S(1)} %pad_maximum_fusion, s32[1024]{0:T(1024)S(1)} %broadcast_clamp_fusion), kind=kCustom, calls=%fused_computation.1 | custom fusion | bytes 1036288 | tf_op jit(solution)/shard_map/gather | solution.py:84
  15.8 21.0 %all-to-all-start = ((bf16[252,64,16]{0,2,1:T(8,128)(2,1)}), bf16[252,64,16]{0,2,1:T(8,128)(2,1)S(1)}, u32[]{:S(2)}, u32[]{:S(2)}) async-start(bf16[252,64,16]{0,2,1:T(8,128)(2,1)} %bitcast.4), calls=%async_computation | async-start | bytes 1048576 | tf_op jit(solution)/shard_map/all_to_all | solution.py:85
  39.1 104.4 %all_gather.11 = bf16[512,512]{1,0:T(8,128)(2,1)} all-gather(bf16[8,512]{1,0:T(8,128)(2,1)S(1)} %copy-done.7), channel_id=1, replica_groups=mesh['member'=4,'node'=64] {'node'}, dimensions={0}, use_global_device_ids=true | all-gather | bytes 532480 | tf_op jit(solution)/shard_map/all_gather | solution.py:77
  143.5 2.2 multiply_convert_fusion.4
  148.4 2.6 fusion.41
  151.0 2.4 convolution_convert_fusion
  154.7 158.7 %while.11 = (s32[]{:T(128)}, f32[640,512]{1,0:T(8,128)}, s32[]{:T(128)}, s32[4096]{0:T(1024)}, s32[]{:T(128)}, /*index=5*/f32[4,4096]{1,0:T(4,128)}, f32[4,512]{...) while((s32[]{:T(128)}, f32[640,512]{1,0:T(8,128)}, ...), condition=%wide.region_3.4_spmd.clone, body=%wide.region_0.3_spmd.clone.sunk | while | flops 1496060416 | bytes 16973068 | solution.py:123
  154.7 1.9 multiply_convert_fusion.6
  158.9 2.6 gather_fusion
  161.5 3.0 convolution_add_fusion.5
  165.2 3.7 %fusion.85 = (f32[512]{0:T(512)S(1)}, f32[512,512]{0,1:T(8,128)}) fusion(bf16[512,512]{1,0:T(8,128)(2,1)} %get-tuple-element.311, f32[512,512]{1,0:T(8,128)} %convolution_add_fusion.5, bf16[640,512]{1,0:T(8,128)(2,1)} %get-tuple-element.310, s32[512]{0:T(512)S(1)} %dynamic_slice.20), kind=kOutput, calls=%fused_computation.65.clone.1 | convolution fusion | flops 606141952 | bytes 3280896 | tf_op jit(solution)/shard_map/while/body/dot_general | solution.py:114
  171.0 3.5 %convolution_add_fusion.6 = f32[640,512]{1,0:T(8,128)} fusion(f32[640,512]{1,0:T(8,128)} %get-tuple-element.281, s32[512]{0:T(512)S(1)} %dynamic_slice.20, f32[512,512]{0,1:T(8,128)} %get-tuple-element.259, f32[512]{0:T(512)S(1)} %bitcast.55, f32[512]{0:T(512)S(1)} %bitcast.54, f32[512]{0:T(512)S(1)} %add_rsqrt_fusion.3, ...), kind=kOutput, calls=%fused_computation.3.clone.1 | convolution fusion | flops 338100224 | bytes 3680768 | tf_op jit(solution)/shard_map/while/body/dot_general | solution.py:118
  174.5 1.9 multiply_convert_fusion.6
  178.7 2.6 gather_fusion
  181.3 3.0 convolution_add_fusion.5
  185.1 3.7 %fusion.85 = (f32[512]{0:T(512)S(1)}, f32[512,512]{0,1:T(8,128)}) fusion(bf16[512,512]{1,0:T(8,128)(2,1)} %get-tuple-element.311, f32[512,512]{1,0:T(8,128)} %convolution_add_fusion.5, bf16[640,512]{1,0:T(8,128)(2,1)} %get-tuple-element.310, s32[512]{0:T(512)S(1)} %dynamic_slice.20), kind=kOutput, calls=%fused_computation.65.clone.1 | convolution fusion | flops 606141952 | bytes 3280896 | tf_op jit(solution)/shard_map/while/body/dot_general | solution.py:114
  190.9 3.5 %convolution_add_fusion.6 = f32[640,512]{1,0:T(8,128)} fusion(f32[640,512]{1,0:T(8,128)} %get-tuple-element.281, s32[512]{0:T(512)S(1)} %dynamic_slice.20, f32[512,512]{0,1:T(8,128)} %get-tuple-element.259, f32[512]{0:T(512)S(1)} %bitcast.55, f32[512]{0:T(512)S(1)} %bitcast.54, f32[512]{0:T(512)S(1)} %add_rsqrt_fusion.3, ...), kind=kOutput, calls=%fused_computation.3.clone.1 | convolution fusion | flops 338100224 | bytes 3680768 | tf_op jit(solution)/shard_map/while/body/dot_general | solution.py:118
  194.4 1.9 multiply_convert_fusion.6
  198.5 2.6 gather_fusion
  201.2 3.0 convolution_add_fusion.5
  204.9 3.7 %fusion.85 = (f32[512]{0:T(512)S(1)}, f32[512,512]{0,1:T(8,128)}) fusion(bf16[512,512]{1,0:T(8,128)(2,1)} %get-tuple-element.311, f32[512,512]{1,0:T(8,128)} %convolution_add_fusion.5, bf16[640,512]{1,0:T(8,128)(2,1)} %get-tuple-element.310, s32[512]{0:T(512)S(1)} %dynamic_slice.20), kind=kOutput, calls=%fused_computation.65.clone.1 | convolution fusion | flops 606141952 | bytes 3280896 | tf_op jit(solution)/shard_map/while/body/dot_general | solution.py:114
  210.7 3.5 %convolution_add_fusion.6 = f32[640,512]{1,0:T(8,128)} fusion(f32[640,512]{1,0:T(8,128)} %get-tuple-element.281, s32[512]{0:T(512)S(1)} %dynamic_slice.20, f32[512,512]{0,1:T(8,128)} %get-tuple-element.259, f32[512]{0:T(512)S(1)} %bitcast.55, f32[512]{0:T(512)S(1)} %bitcast.54, f32[512]{0:T(512)S(1)} %add_rsqrt_fusion.3, ...), kind=kOutput, calls=%fused_computation.3.clone.1 | convolution fusion | flops 338100224 | bytes 3680768 | tf_op jit(solution)/shard_map/while/body/dot_general | solution.py:118
  214.2 1.9 multiply_convert_fusion.6
  218.4 2.6 gather_fusion
  221.0 3.0 convolution_add_fusion.5
  224.8 3.7 %fusion.85 = (f32[512]{0:T(512)S(1)}, f32[512,512]{0,1:T(8,128)}) fusion(bf16[512,512]{1,0:T(8,128)(2,1)} %get-tuple-element.311, f32[512,512]{1,0:T(8,128)} %convolution_add_fusion.5, bf16[640,512]{1,0:T(8,128)(2,1)} %get-tuple-element.310, s32[512]{0:T(512)S(1)} %dynamic_slice.20), kind=kOutput, calls=%fused_computation.65.clone.1 | convolution fusion | flops 606141952 | bytes 3280896 | tf_op jit(solution)/shard_map/while/body/dot_general | solution.py:114
  230.5 3.5 %convolution_add_fusion.6 = f32[640,512]{1,0:T(8,128)} fusion(f32[640,512]{1,0:T(8,128)} %get-tuple-element.281, s32[512]{0:T(512)S(1)} %dynamic_slice.20, f32[512,512]{0,1:T(8,128)} %get-tuple-element.259, f32[512]{0:T(512)S(1)} %bitcast.55, f32[512]{0:T(512)S(1)} %bitcast.54, f32[512]{0:T(512)S(1)} %add_rsqrt_fusion.3, ...), kind=kOutput, calls=%fused_computation.3.clone.1 | convolution fusion | flops 338100224 | bytes 3680768 | tf_op jit(solution)/shard_map/while/body/dot_general | solution.py:118
  238.2 2.6 gather_fusion
  240.8 3.0 convolution_add_fusion.5
  244.6 3.7 %fusion.85 = (f32[512]{0:T(512)S(1)}, f32[512,512]{0,1:T(8,128)}) fusion(bf16[512,512]{1,0:T(8,128)(2,1)} %get-tuple-element.311, f32[512,512]{1,0:T(8,128)} %convolution_add_fusion.5, bf16[640,512]{1,0:T(8,128)(2,1)} %get-tuple-element.310, s32[512]{0:T(512)S(1)} %dynamic_slice.20), kind=kOutput, calls=%fused_computation.65.clone.1 | convolution fusion | flops 606141952 | bytes 3280896 | tf_op jit(solution)/shard_map/while/body/dot_general | solution.py:114
  250.4 3.5 %convolution_add_fusion.6 = f32[640,512]{1,0:T(8,128)} fusion(f32[640,512]{1,0:T(8,128)} %get-tuple-element.281, s32[512]{0:T(512)S(1)} %dynamic_slice.20, f32[512,512]{0,1:T(8,128)} %get-tuple-element.259, f32[512]{0:T(512)S(1)} %bitcast.55, f32[512]{0:T(512)S(1)} %bitcast.54, f32[512]{0:T(512)S(1)} %add_rsqrt_fusion.3, ...), kind=kOutput, calls=%fused_computation.3.clone.1 | convolution fusion | flops 338100224 | bytes 3680768 | tf_op jit(solution)/shard_map/while/body/dot_general | solution.py:118
  253.9 1.9 multiply_convert_fusion.6
  258.1 2.6 gather_fusion
  260.7 3.0 convolution_add_fusion.5
  264.4 3.7 %fusion.85 = (f32[512]{0:T(512)S(1)}, f32[512,512]{0,1:T(8,128)}) fusion(bf16[512,512]{1,0:T(8,128)(2,1)} %get-tuple-element.311, f32[512,512]{1,0:T(8,128)} %convolution_add_fusion.5, bf16[640,512]{1,0:T(8,128)(2,1)} %get-tuple-element.310, s32[512]{0:T(512)S(1)} %dynamic_slice.20), kind=kOutput, calls=%fused_computation.65.clone.1 | convolution fusion | flops 606141952 | bytes 3280896 | tf_op jit(solution)/shard_map/while/body/dot_general | solution.py:114
  270.2 3.5 %convolution_add_fusion.6 = f32[640,512]{1,0:T(8,128)} fusion(f32[640,512]{1,0:T(8,128)} %get-tuple-element.281, s32[512]{0:T(512)S(1)} %dynamic_slice.20, f32[512,512]{0,1:T(8,128)} %get-tuple-element.259, f32[512]{0:T(512)S(1)} %bitcast.55, f32[512]{0:T(512)S(1)} %bitcast.54, f32[512]{0:T(512)S(1)} %add_rsqrt_fusion.3, ...), kind=kOutput, calls=%fused_computation.3.clone.1 | convolution fusion | flops 338100224 | bytes 3680768 | tf_op jit(solution)/shard_map/while/body/dot_general | solution.py:118
  273.7 1.9 multiply_convert_fusion.6
  277.9 2.6 gather_fusion
  280.5 3.0 convolution_add_fusion.5
  284.3 3.7 %fusion.85 = (f32[512]{0:T(512)S(1)}, f32[512,512]{0,1:T(8,128)}) fusion(bf16[512,512]{1,0:T(8,128)(2,1)} %get-tuple-element.311, f32[512,512]{1,0:T(8,128)} %convolution_add_fusion.5, bf16[640,512]{1,0:T(8,128)(2,1)} %get-tuple-element.310, s32[512]{0:T(512)S(1)} %dynamic_slice.20), kind=kOutput, calls=%fused_computation.65.clone.1 | convolution fusion | flops 606141952 | bytes 3280896 | tf_op jit(solution)/shard_map/while/body/dot_general | solution.py:114
  290.0 3.5 %convolution_add_fusion.6 = f32[640,512]{1,0:T(8,128)} fusion(f32[640,512]{1,0:T(8,128)} %get-tuple-element.281, s32[512]{0:T(512)S(1)} %dynamic_slice.20, f32[512,512]{0,1:T(8,128)} %get-tuple-element.259, f32[512]{0:T(512)S(1)} %bitcast.55, f32[512]{0:T(512)S(1)} %bitcast.54, f32[512]{0:T(512)S(1)} %add_rsqrt_fusion.3, ...), kind=kOutput, calls=%fused_computation.3.clone.1 | convolution fusion | flops 338100224 | bytes 3680768 | tf_op jit(solution)/shard_map/while/body/dot_general | solution.py:118
  297.7 2.6 gather_fusion
  300.3 3.0 convolution_add_fusion.5
  304.1 3.7 %fusion.85 = (f32[512]{0:T(512)S(1)}, f32[512,512]{0,1:T(8,128)}) fusion(bf16[512,512]{1,0:T(8,128)(2,1)} %get-tuple-element.311, f32[512,512]{1,0:T(8,128)} %convolution_add_fusion.5, bf16[640,512]{1,0:T(8,128)(2,1)} %get-tuple-element.310, s32[512]{0:T(512)S(1)} %dynamic_slice.20), kind=kOutput, calls=%fused_computation.65.clone.1 | convolution fusion | flops 606141952 | bytes 3280896 | tf_op jit(solution)/shard_map/while/body/dot_general | solution.py:114
  309.9 3.5 %convolution_add_fusion.6 = f32[640,512]{1,0:T(8,128)} fusion(f32[640,512]{1,0:T(8,128)} %get-tuple-element.281, s32[512]{0:T(512)S(1)} %dynamic_slice.20, f32[512,512]{0,1:T(8,128)} %get-tuple-element.259, f32[512]{0:T(512)S(1)} %bitcast.55, f32[512]{0:T(512)S(1)} %bitcast.54, f32[512]{0:T(512)S(1)} %add_rsqrt_fusion.3, ...), kind=kOutput, calls=%fused_computation.3.clone.1 | convolution fusion | flops 338100224 | bytes 3680768 | tf_op jit(solution)/shard_map/while/body/dot_general | solution.py:118
  313.4 2.4 copy.40
  315.8 3.9 %fusion.42 = (f32[640]{0:T(1024)S(1)}, f32[640,512]{0,1:T(8,128)S(1)}) fusion(bf16[512,512]{1,0:T(8,128)(2,1)} %all_gather.11, bf16[1024,512]{1,0:T(8,128)(2,1)} %all-gather.5.cloned.1.call-done, bf16[640,512]{0,1:T(8,128)(2,1)} %copy.40, bf16[640,512]{0,1:T(8,128)(2,1)} %multiply_convert_fusion.4), kind=kOutput, calls=%fused_computation.67 | convolution fusion | flops 1011219840 | bytes 4196864 | tf_op jit(solution)/shard_map/dot_general | solution.py:129
  322.0 2.2 copy.43
  (140 shorter events, 55.2 us)
Async XLA Ops:
  6.5 32.1 %copy-start = (bf16[512,2048]{1,0:T(8,128)(2,1)S(1)}, bf16[512,2048]{1,0:T(8,128)(2,1)}, u32[]{:S(2)}) copy-start(bf16[512,2048]{1,0:T(8,128)(2,1)} %param.43) | copy-start | bytes 6291460
  6.6 3.6 %copy-start.5 = (bf16[168,1024]{1,0:T(8,128)(2,1)S(1)}, bf16[168,1024]{1,0:T(8,128)(2,1)}, u32[]{:S(2)}) copy-start(bf16[168,1024]{1,0:T(8,128)(2,1)} %param.23) | copy-start | bytes 1032196
  6.6 3.9 %copy-start.8 = (s32[64,16]{0,1:T(8,128)S(1)}, s32[64,16]{0,1:T(8,128)}, u32[]{:S(2)}) copy-start(s32[64,16]{0,1:T(8,128)} %param.31) | copy-start | bytes 12292
  6.6 141.8 %all-gather.3.cloned.1.call-start = ((), (), s32[]{:S(2)}) async-start(), calls=%async_computation.1 | async-start | bytes 2129920 | tf_op jit(solution)/shard_map/all_gather | solution.py:16
  10.8 27.6 %copy-start.6 = (f32[32,512]{1,0:T(8,128)S(1)}, f32[32,512]{1,0:T(8,128)}, u32[]{:S(2)}) copy-start(f32[32,512]{1,0:T(8,128)} %param.42) | copy-start | bytes 196612
  15.8 129.9 %all-to-all-start = ((bf16[252,64,16]{0,2,1:T(8,128)(2,1)}), bf16[252,64,16]{0,2,1:T(8,128)(2,1)S(1)}, u32[]{:S(2)}, u32[]{:S(2)}) async-start(bf16[252,64,16]{0,2,1:T(8,128)(2,1)} %bitcast.4), calls=%async_computation | async-start | bytes 1048576 | tf_op jit(solution)/shard_map/all_to_all | solution.py:85
  36.8 2.3 copy-start.7
  36.8 279.0 %all-gather.5.cloned.1.call-start = ((), (), s32[]{:S(2)}) async-start(), calls=%async_computation.2 | async-start | bytes 1064960 | tf_op jit(solution)/shard_map/all_gather | solution.py:76
  38.7 104.8 %copy-start.9 = (f32[3,640]{1,0:T(4,128)S(1)}, f32[3,640]{1,0:T(4,128)}, u32[]{:S(2)}) copy-start(f32[3,640]{1,0:T(4,128)} %param.27) | copy-start | bytes 23044
  38.7 104.8 %copy-start.10 = (f32[3,512]{1,0:T(4,128)S(1)}, f32[3,512]{1,0:T(4,128)}, u32[]{:S(2)}) copy-start(f32[3,512]{1,0:T(4,128)} %param.34) | copy-start | bytes 18436
  145.7 0.8 copy-start.4
  148.4 2.6 copy-start.2
  151.0 3.7 %copy-start.11 = (f32[4,512]{1,0:T(4,128)S(1)}, f32[4,512]{1,0:T(4,128)}, u32[]{:S(2)}) copy-start(f32[4,512]{1,0:T(4,128)} %param.35) | copy-start | bytes 24580
  154.7 1.9 copy-start.1
  174.5 1.9 copy-start.1
  194.4 1.9 copy-start.1
  214.2 1.9 copy-start.1
  234.1 1.9 copy-start.1
  253.9 1.9 copy-start.1
  273.7 1.9 copy-start.1
  293.6 1.9 copy-start.1
  319.7 1.1 copy-start.3
Sparse Core Ops, SparseCore 0:
  9.2 137.0 all-gather.2
  148.2 123.3 all-gather.4
where the time goes:
time: 333 us; the launch traced here: 331 us
  matrix products  120 us (36%)
  blocking collectives  104 us (31%)
  local copies, waits for them, and re-layouts  42.7 us (13%)
  other arithmetic  26.8 us (8%)
  starting transfers between devices  21.1 us (6%)
  between operations  15.1 us (5%)
    all_gather x1, blocking collectives, per_device(): lax.all_gather(output_weight, 'node', axis=0, tiled=True)  104 us
    dot_general x8, matrix products, add_block(): mixed = jnp.dot(hidden, full_message, preferred_element_type=jnp.float32)  29.9 us
    dot_general x8, matrix products, add_block(): lax.dot_general(one_hot, message, (((0,), (0,)), ((), ())), preferred_ele...  28 us
    dot_general x8, matrix products, add_block(): jnp.dot(sender_rows, full_sender, preferred_element_type=jnp.float32)  24 us
    all_to_all x1, starting transfers between devices, per_device(): lax.all_to_all(outgoing_inputs, 'node', split_axis=1, concat_axis=1, tile...  21 us
    gather x8, local copies, waits for them, and re-layouts, add_block(): sender_rows = received[slots]  20.9 us
    dot_general x8, matrix products, add_block(): jnp.dot(geometry.T, geom_weight, precision=lax.Precision.HIGHEST)  15.4 us
    dot_general x8, matrix products, add_block(): pre = jnp.dot(embed_rows, full_edge, preferred_element_type=jnp.float32)  11.6 us
  transfers between devices with their start and end apart: 3, of which 0 were waited for; matrix products, arithmetic and copies ran while one was open for 54% of the time, Pallas kernels for 0%

commit v1 on v0

--- a/solution.py
+++ b/solution.py
@@ -74,7 +74,9 @@
     full_sender, full_edge, full_recv, full_message, full_node, full_output = (
         *in_one_piece((sender_weight, edge_weight, receiver_weight, message_weight), "node", 0, 1),
         lax.all_gather(node_weight, "node", axis=0, tiled=True),
-        lax.all_gather(output_weight, "node", axis=0, tiled=True),
+        jnp.concatenate(
+            lax.all_to_all(jnp.stack([output_weight] * lax.axis_size("node")), "node", 0, 0), axis=0
+        ),
     )
     noisy = ((target_state + sigma * noise_sample) / jnp.sqrt(sigma * sigma + 1.0)).astype(
         jnp.bfloat16

time: 333 us -> 346 us (1.039)
  blocking collectives: 104 us -> 0 us
  waiting for transfers between devices: 0.81 us -> 93.4 us
  starting transfers between devices: 21.1 us -> 44 us
    all_gather x1 -> x0, blocking collectives: 104 us -> none  [per_device(): lax.all_gather(output_weight, 'node', axis=0, tiled=True)]
    all_to_all x1, waiting for transfers between devices: 0.01 us -> 48.1 us  [per_device(): lax.all_to_all(outgoing_inputs, 'node', split_axis=1, concat_axis=1, tile...]
    all_gather x1, waiting for transfers between devices: 0.02 us -> 44.6 us  [in_one_piece(): out = lax.all_gather(both, axis, axis=dim, tiled=True)]
    all_to_all x0 -> x1, starting transfers between devices: none -> 23 us  [per_device(): lax.all_to_all(jnp.stack([output_weight] * lax.axis_size('node')), 'node'...]
  transfers between devices with their start and end apart: 3 -> 4, of which waited for: 0 -> 2; matrix products, arithmetic and copies ran while one was open for 54% -> 52% of each run, Pallas kernels for 0% -> 0%
where the time goes in v1:
time: 346 us; the launch traced here: 342 us
  matrix products  120 us (35%)
  waiting for transfers between devices  93.4 us (27%)
  starting transfers between devices  44 us (13%)
  local copies, waits for them, and re-layouts  42.8 us (12%)
  other arithmetic  26.8 us (8%)
  between operations  15.1 us (4%)
    all_to_all x1, waiting for transfers between devices, per_device(): lax.all_to_all(outgoing_inputs, 'node', split_axis=1, concat_axis=1, tile...  48.1 us
    all_gather x1, waiting for transfers between devices, in_one_piece(): out = lax.all_gather(both, axis, axis=dim, tiled=True)  44.6 us
    dot_general x8, matrix products, add_block(): mixed = jnp.dot(hidden, full_message, preferred_element_type=jnp.float32)  29.8 us
    dot_general x8, matrix products, add_block(): lax.dot_general(one_hot, message, (((0,), (0,)), ((), ())), preferred_ele...  28 us
    dot_general x8, matrix products, add_block(): jnp.dot(sender_rows, full_sender, preferred_element_type=jnp.float32)  23.8 us
    all_to_all x1, starting transfers between devices, per_device(): lax.all_to_all(jnp.stack([output_weight] * lax.axis_size('node')), 'node'...  23 us
    all_to_all x1, starting transfers between devices, per_device(): lax.all_to_all(outgoing_inputs, 'node', split_axis=1, concat_axis=1, tile...  21 us
    gather x8, local copies, waits for them, and re-layouts, add_block(): sender_rows = received[slots]  21 us
  transfers between devices with their start and end apart: 4, of which 2 were waited for; matrix products, arithmetic and copies ran while one was open for 52% of the time, Pallas kernels for 0%

profile of v1, /device:TPU:1325, one launch (start us, length us, event | category | flops | bytes accessed | tf_op | source)
XLA Modules:
  0.0 341.9 jit_solution(12078315149600516588)
XLA Ops:
  10.8 5.0 %gather_fusion.1 = bf16[1024,252]{1,0:T(8,128)(2,1)} fusion(bf16[252,1024]{0,1:T(8,128)(2,1)S(1)} %pad_maximum_fusion, s32[1024]{0:T(1024)S(1)} %broadcast_clamp_fusion), kind=kCustom, calls=%fused_computation.1 | custom fusion | bytes 1036288 | tf_op jit(solution)/shard_map/gather | solution.py:86
  15.8 21.0 %all-to-all-start = ((bf16[252,64,16]{0,2,1:T(8,128)(2,1)}), bf16[252,64,16]{0,2,1:T(8,128)(2,1)S(1)}, u32[]{:S(2)}, u32[]{:S(2)}) async-start(bf16[252,64,16]{0,2,1:T(8,128)(2,1)} %bitcast.4), calls=%async_computation | async-start | bytes 1048576 | tf_op jit(solution)/shard_map/all_to_all | solution.py:87
  39.0 2.2 multiply_convert_fusion.4
  41.3 48.1 %all-to-all-done = bf16[252,64,16]{0,2,1:T(8,128)(2,1)S(1)} async-done(((bf16[252,64,16]{0,2,1:T(8,128)(2,1)}), bf16[252,64,16]{0,2,1:T(8,128)(2,1)S(1)}, u32[]{:S(2)}, u32[]{:S(2)}) %all-to-all-start) | async-done | bytes 516128 | tf_op jit(solution)/shard_map/all_to_all | solution.py:87
  90.3 23.0 %all-to-all-start.1 = ((bf16[64,8,512]{2,1,0:T(8,128)(2,1)}), bf16[64,8,512]{2,1,0:T(8,128)(2,1)}, u32[]{:S(2)}, u32[]{:S(2)}) async-start(bf16[64,8,512]{2,1,0:T(8,128)(2,1)} %stack.2), calls=%async_computation.1 | async-start | bytes 1048576 | tf_op jit(solution)/shard_map/all_to_all | solution.py:78
  115.1 44.6 %all-gather.3.cloned.1.call-done = bf16[512,2048]{1,0:T(8,128)(2,1)} async-done(((bf16[8,2048]{1,0:T(8,128)(2,1)}), bf16[512,2048]{1,0:T(8,128)(2,1)}) %all-gather.3.cloned.1.call-update) | async-done | bytes 2097168 | tf_op jit(solution)/shard_map/all_gather | solution.py:16
  159.7 2.6 fusion.42
  162.3 2.4 convolution_convert_fusion
  166.0 158.4 %while.11 = (s32[]{:T(128)}, f32[640,512]{1,0:T(8,128)}, s32[]{:T(128)}, s32[4096]{0:T(1024)}, s32[]{:T(128)}, /*index=5*/f32[4,4096]{1,0:T(4,128)}, f32[4,512]{...) while((s32[]{:T(128)}, f32[640,512]{1,0:T(8,128)}, ...), condition=%wide.region_3.4_spmd.clone, body=%wide.region_0.3_spmd.clone.sunk | while | flops 1496060416 | bytes 16973068 | solution.py:125
  170.1 2.6 gather_fusion
  172.7 3.0 convolution_add_fusion.5
  176.5 3.7 %fusion.85 = (f32[512]{0:T(512)S(1)}, f32[512,512]{0,1:T(8,128)}) fusion(bf16[512,512]{1,0:T(8,128)(2,1)} %get-tuple-element.311, f32[512,512]{1,0:T(8,128)} %convolution_add_fusion.5, bf16[640,512]{1,0:T(8,128)(2,1)} %get-tuple-element.310, s32[512]{0:T(512)S(1)} %dynamic_slice.20), kind=kOutput, calls=%fused_computation.66.clone.1 | convolution fusion | flops 606141952 | bytes 3280896 | tf_op jit(solution)/shard_map/while/body/dot_general | solution.py:116
  182.3 3.5 %convolution_add_fusion.6 = f32[640,512]{1,0:T(8,128)} fusion(f32[640,512]{1,0:T(8,128)} %get-tuple-element.281, s32[512]{0:T(512)S(1)} %dynamic_slice.20, f32[512,512]{0,1:T(8,128)} %get-tuple-element.259, f32[512]{0:T(512)S(1)} %bitcast.59, f32[512]{0:T(512)S(1)} %bitcast.58, f32[512]{0:T(512)S(1)} %add_rsqrt_fusion.3, ...), kind=kOutput, calls=%fused_computation.3.clone.1 | convolution fusion | flops 338100224 | bytes 3680768 | tf_op jit(solution)/shard_map/while/body/dot_general | solution.py:120
  185.8 1.9 multiply_convert_fusion.6
  189.9 2.6 gather_fusion
  192.5 3.0 convolution_add_fusion.5
  196.3 3.7 %fusion.85 = (f32[512]{0:T(512)S(1)}, f32[512,512]{0,1:T(8,128)}) fusion(bf16[512,512]{1,0:T(8,128)(2,1)} %get-tuple-element.311, f32[512,512]{1,0:T(8,128)} %convolution_add_fusion.5, bf16[640,512]{1,0:T(8,128)(2,1)} %get-tuple-element.310, s32[512]{0:T(512)S(1)} %dynamic_slice.20), kind=kOutput, calls=%fused_computation.66.clone.1 | convolution fusion | flops 606141952 | bytes 3280896 | tf_op jit(solution)/shard_map/while/body/dot_general | solution.py:116
  202.1 3.5 %convolution_add_fusion.6 = f32[640,512]{1,0:T(8,128)} fusion(f32[640,512]{1,0:T(8,128)} %get-tuple-element.281, s32[512]{0:T(512)S(1)} %dynamic_slice.20, f32[512,512]{0,1:T(8,128)} %get-tuple-element.259, f32[512]{0:T(512)S(1)} %bitcast.59, f32[512]{0:T(512)S(1)} %bitcast.58, f32[512]{0:T(512)S(1)} %add_rsqrt_fusion.3, ...), kind=kOutput, calls=%fused_computation.3.clone.1 | convolution fusion | flops 338100224 | bytes 3680768 | tf_op jit(solution)/shard_map/while/body/dot_general | solution.py:120
  209.7 2.6 gather_fusion
  212.3 3.0 convolution_add_fusion.5
  216.1 3.7 %fusion.85 = (f32[512]{0:T(512)S(1)}, f32[512,512]{0,1:T(8,128)}) fusion(bf16[512,512]{1,0:T(8,128)(2,1)} %get-tuple-element.311, f32[512,512]{1,0:T(8,128)} %convolution_add_fusion.5, bf16[640,512]{1,0:T(8,128)(2,1)} %get-tuple-element.310, s32[512]{0:T(512)S(1)} %dynamic_slice.20), kind=kOutput, calls=%fused_computation.66.clone.1 | convolution fusion | flops 606141952 | bytes 3280896 | tf_op jit(solution)/shard_map/while/body/dot_general | solution.py:116
  221.9 3.5 %convolution_add_fusion.6 = f32[640,512]{1,0:T(8,128)} fusion(f32[640,512]{1,0:T(8,128)} %get-tuple-element.281, s32[512]{0:T(512)S(1)} %dynamic_slice.20, f32[512,512]{0,1:T(8,128)} %get-tuple-element.259, f32[512]{0:T(512)S(1)} %bitcast.59, f32[512]{0:T(512)S(1)} %bitcast.58, f32[512]{0:T(512)S(1)} %add_rsqrt_fusion.3, ...), kind=kOutput, calls=%fused_computation.3.clone.1 | convolution fusion | flops 338100224 | bytes 3680768 | tf_op jit(solution)/shard_map/while/body/dot_general | solution.py:120
  225.4 1.9 multiply_convert_fusion.6
  229.5 2.6 gather_fusion
  232.1 3.0 convolution_add_fusion.5
  235.9 3.7 %fusion.85 = (f32[512]{0:T(512)S(1)}, f32[512,512]{0,1:T(8,128)}) fusion(bf16[512,512]{1,0:T(8,128)(2,1)} %get-tuple-element.311, f32[512,512]{1,0:T(8,128)} %convolution_add_fusion.5, bf16[640,512]{1,0:T(8,128)(2,1)} %get-tuple-element.310, s32[512]{0:T(512)S(1)} %dynamic_slice.20), kind=kOutput, calls=%fused_computation.66.clone.1 | convolution fusion | flops 606141952 | bytes 3280896 | tf_op jit(solution)/shard_map/while/body/dot_general | solution.py:116
  241.7 3.5 %convolution_add_fusion.6 = f32[640,512]{1,0:T(8,128)} fusion(f32[640,512]{1,0:T(8,128)} %get-tuple-element.281, s32[512]{0:T(512)S(1)} %dynamic_slice.20, f32[512,512]{0,1:T(8,128)} %get-tuple-element.259, f32[512]{0:T(512)S(1)} %bitcast.59, f32[512]{0:T(512)S(1)} %bitcast.58, f32[512]{0:T(512)S(1)} %add_rsqrt_fusion.3, ...), kind=kOutput, calls=%fused_computation.3.clone.1 | convolution fusion | flops 338100224 | bytes 3680768 | tf_op jit(solution)/shard_map/while/body/dot_general | solution.py:120
  245.2 1.9 multiply_convert_fusion.6
  249.3 2.6 gather_fusion
  251.9 3.0 convolution_add_fusion.5
  255.7 3.7 %fusion.85 = (f32[512]{0:T(512)S(1)}, f32[512,512]{0,1:T(8,128)}) fusion(bf16[512,512]{1,0:T(8,128)(2,1)} %get-tuple-element.311, f32[512,512]{1,0:T(8,128)} %convolution_add_fusion.5, bf16[640,512]{1,0:T(8,128)(2,1)} %get-tuple-element.310, s32[512]{0:T(512)S(1)} %dynamic_slice.20), kind=kOutput, calls=%fused_computation.66.clone.1 | convolution fusion | flops 606141952 | bytes 3280896 | tf_op jit(solution)/shard_map/while/body/dot_general | solution.py:116
  261.5 3.5 %convolution_add_fusion.6 = f32[640,512]{1,0:T(8,128)} fusion(f32[640,512]{1,0:T(8,128)} %get-tuple-element.281, s32[512]{0:T(512)S(1)} %dynamic_slice.20, f32[512,512]{0,1:T(8,128)} %get-tuple-element.259, f32[512]{0:T(512)S(1)} %bitcast.59, f32[512]{0:T(512)S(1)} %bitcast.58, f32[512]{0:T(512)S(1)} %add_rsqrt_fusion.3, ...), kind=kOutput, calls=%fused_computation.3.clone.1 | convolution fusion | flops 338100224 | bytes 3680768 | tf_op jit(solution)/shard_map/while/body/dot_general | solution.py:120
  265.0 1.9 multiply_convert_fusion.6
  269.1 2.6 gather_fusion
  271.7 3.0 convolution_add_fusion.5
  275.5 3.7 %fusion.85 = (f32[512]{0:T(512)S(1)}, f32[512,512]{0,1:T(8,128)}) fusion(bf16[512,512]{1,0:T(8,128)(2,1)} %get-tuple-element.311, f32[512,512]{1,0:T(8,128)} %convolution_add_fusion.5, bf16[640,512]{1,0:T(8,128)(2,1)} %get-tuple-element.310, s32[512]{0:T(512)S(1)} %dynamic_slice.20), kind=kOutput, calls=%fused_computation.66.clone.1 | convolution fusion | flops 606141952 | bytes 3280896 | tf_op jit(solution)/shard_map/while/body/dot_general | solution.py:116
  281.2 3.5 %convolution_add_fusion.6 = f32[640,512]{1,0:T(8,128)} fusion(f32[640,512]{1,0:T(8,128)} %get-tuple-element.281, s32[512]{0:T(512)S(1)} %dynamic_slice.20, f32[512,512]{0,1:T(8,128)} %get-tuple-element.259, f32[512]{0:T(512)S(1)} %bitcast.59, f32[512]{0:T(512)S(1)} %bitcast.58, f32[512]{0:T(512)S(1)} %add_rsqrt_fusion.3, ...), kind=kOutput, calls=%fused_computation.3.clone.1 | convolution fusion | flops 338100224 | bytes 3680768 | tf_op jit(solution)/shard_map/while/body/dot_general | solution.py:120
  288.9 2.6 gather_fusion
  291.5 3.0 convolution_add_fusion.5
  295.3 3.7 %fusion.85 = (f32[512]{0:T(512)S(1)}, f32[512,512]{0,1:T(8,128)}) fusion(bf16[512,512]{1,0:T(8,128)(2,1)} %get-tuple-element.311, f32[512,512]{1,0:T(8,128)} %convolution_add_fusion.5, bf16[640,512]{1,0:T(8,128)(2,1)} %get-tuple-element.310, s32[512]{0:T(512)S(1)} %dynamic_slice.20), kind=kOutput, calls=%fused_computation.66.clone.1 | convolution fusion | flops 606141952 | bytes 3280896 | tf_op jit(solution)/shard_map/while/body/dot_general | solution.py:116
  301.0 3.5 %convolution_add_fusion.6 = f32[640,512]{1,0:T(8,128)} fusion(f32[640,512]{1,0:T(8,128)} %get-tuple-element.281, s32[512]{0:T(512)S(1)} %dynamic_slice.20, f32[512,512]{0,1:T(8,128)} %get-tuple-element.259, f32[512]{0:T(512)S(1)} %bitcast.59, f32[512]{0:T(512)S(1)} %bitcast.58, f32[512]{0:T(512)S(1)} %add_rsqrt_fusion.3, ...), kind=kOutput, calls=%fused_computation.3.clone.1 | convolution fusion | flops 338100224 | bytes 3680768 | tf_op jit(solution)/shard_map/while/body/dot_general | solution.py:120
  308.7 2.6 gather_fusion
  311.3 3.0 convolution_add_fusion.5
  315.0 3.7 %fusion.85 = (f32[512]{0:T(512)S(1)}, f32[512,512]{0,1:T(8,128)}) fusion(bf16[512,512]{1,0:T(8,128)(2,1)} %get-tuple-element.311, f32[512,512]{1,0:T(8,128)} %convolution_add_fusion.5, bf16[640,512]{1,0:T(8,128)(2,1)} %get-tuple-element.310, s32[512]{0:T(512)S(1)} %dynamic_slice.20), kind=kOutput, calls=%fused_computation.66.clone.1 | convolution fusion | flops 606141952 | bytes 3280896 | tf_op jit(solution)/shard_map/while/body/dot_general | solution.py:116
  320.8 3.5 %convolution_add_fusion.6 = f32[640,512]{1,0:T(8,128)} fusion(f32[640,512]{1,0:T(8,128)} %get-tuple-element.281, s32[512]{0:T(512)S(1)} %dynamic_slice.20, f32[512,512]{0,1:T(8,128)} %get-tuple-element.259, f32[512]{0:T(512)S(1)} %bitcast.59, f32[512]{0:T(512)S(1)} %bitcast.58, f32[512]{0:T(512)S(1)} %add_rsqrt_fusion.3, ...), kind=kOutput, calls=%fused_computation.3.clone.1 | convolution fusion | flops 338100224 | bytes 3680768 | tf_op jit(solution)/shard_map/while/body/dot_general | solution.py:120
  324.3 2.4 copy.40
  326.7 3.9 %fusion.43 = (f32[640]{0:T(1024)S(1)}, f32[640,512]{0,1:T(8,128)S(1)}) fusion(bf16[64,8,512]{2,1,0:T(8,128)(2,1)} %all-to-all-done.1, bf16[1024,512]{1,0:T(8,128)(2,1)} %all-gather.5.cloned.1.call-done, bf16[640,512]{0,1:T(8,128)(2,1)} %copy.40, bf16[640,512]{0,1:T(8,128)(2,1)} %multiply_convert_fusion.4), kind=kOutput, calls=%fused_computation.68 | convolution fusion | flops 1011219840 | bytes 4196864 | tf_op jit(solution)/shard_map/dot_general | solution.py:131
  332.9 2.2 copy.43
  (142 shorter events, 59.0 us)
Async XLA Ops:
  6.5 32.1 %copy-start = (bf16[512,2048]{1,0:T(8,128)(2,1)S(1)}, bf16[512,2048]{1,0:T(8,128)(2,1)}, u32[]{:S(2)}) copy-start(bf16[512,2048]{1,0:T(8,128)(2,1)} %param.43) | copy-start | bytes 6291460
  6.6 3.6 %copy-start.5 = (bf16[168,1024]{1,0:T(8,128)(2,1)S(1)}, bf16[168,1024]{1,0:T(8,128)(2,1)}, u32[]{:S(2)}) copy-start(bf16[168,1024]{1,0:T(8,128)(2,1)} %param.23) | copy-start | bytes 1032196
  6.6 3.9 %copy-start.8 = (s32[64,16]{0,1:T(8,128)S(1)}, s32[64,16]{0,1:T(8,128)}, u32[]{:S(2)}) copy-start(s32[64,16]{0,1:T(8,128)} %param.31) | copy-start | bytes 12292
  6.6 153.1 %all-gather.3.cloned.1.call-start = ((), (), s32[]{:S(2)}) async-start(), calls=%async_computation.2 | async-start | bytes 2129920 | tf_op jit(solution)/shard_map/all_gather | solution.py:16
  10.8 27.6 %copy-start.6 = (f32[32,512]{1,0:T(8,128)S(1)}, f32[32,512]{1,0:T(8,128)}, u32[]{:S(2)}) copy-start(f32[32,512]{1,0:T(8,128)} %param.42) | copy-start | bytes 196612
  15.8 73.6 %all-to-all-start = ((bf16[252,64,16]{0,2,1:T(8,128)(2,1)}), bf16[252,64,16]{0,2,1:T(8,128)(2,1)S(1)}, u32[]{:S(2)}, u32[]{:S(2)}) async-start(bf16[252,64,16]{0,2,1:T(8,128)(2,1)} %bitcast.4), calls=%async_computation | async-start | bytes 1048576 | tf_op jit(solution)/shard_map/all_to_all | solution.py:87
  36.8 2.3 copy-start.9
  36.8 2.3 copy-start.10
  36.8 289.9 %all-gather.5.cloned.1.call-start = ((), (), s32[]{:S(2)}) async-start(), calls=%async_computation.3 | async-start | bytes 1064960 | tf_op jit(solution)/shard_map/all_gather | solution.py:76
  39.0 50.3 %copy-start.7 = (bf16[8,512]{1,0:T(8,128)(2,1)S(1)}, bf16[8,512]{1,0:T(8,128)(2,1)}, u32[]{:S(2)}) copy-start(bf16[8,512]{1,0:T(8,128)(2,1)} %param.41) | copy-start | bytes 24580
  89.4 23.9 %copy-start.4 = (bf16[252,64,16]{0,2,1:T(8,128)(2,1)}, bf16[252,64,16]{0,2,1:T(8,128)(2,1)S(1)}, u32[]{:S(2)}) copy-start(bf16[252,64,16]{0,2,1:T(8,128)(2,1)S(1)} %all-to-all-done) | copy-start | bytes 1548292
  90.3 236.5 %all-to-all-start.1 = ((bf16[64,8,512]{2,1,0:T(8,128)(2,1)}), bf16[64,8,512]{2,1,0:T(8,128)(2,1)}, u32[]{:S(2)}, u32[]{:S(2)}) async-start(bf16[64,8,512]{2,1,0:T(8,128)(2,1)} %stack.2), calls=%async_computation.1 | async-start | bytes 1048576 | tf_op jit(solution)/shard_map/all_to_all | solution.py:78
  159.6 2.6 copy-start.2
  162.3 3.7 %copy-start.11 = (f32[4,512]{1,0:T(4,128)S(1)}, f32[4,512]{1,0:T(4,128)}, u32[]{:S(2)}) copy-start(f32[4,512]{1,0:T(4,128)} %param.35) | copy-start | bytes 24580
  166.0 1.9 copy-start.1
  185.8 1.9 copy-start.1
  205.6 1.9 copy-start.1
  225.4 1.9 copy-start.1
  245.2 1.9 copy-start.1
  265.0 1.9 copy-start.1
  284.8 1.9 copy-start.1
  304.5 1.9 copy-start.1
  330.6 1.1 copy-start.3
Sparse Core Ops, SparseCore 0:
  9.2 150.4 all-gather.2
  161.5 123.6 all-gather.4
